TPU v7x, 32 devices: a whole 2x2x4 slice. The times are simulated.
32 devices in a mesh: seq: 2 (over x), shard: 16 (over z, y, core).
Axes of the slice: x: 2, y: 2, z: 4, core: 2. Of those that a mesh axis runs over, the one named last changes fastest.
Arguments:
- hidden_in: bfloat16 [16, 1024, 768], P('shard', 'seq'), may hold values from -6 to 6
- encoded: bfloat16 [16, 1024, 768], P('shard', 'seq'), may hold values from -6 to 6
- cotangent: bfloat16 [16, 1024, 768], P('shard', 'seq'), may hold values from -6 to 6
- buckets: int32 [1024], replicated, may hold values from 0 to 31, as said below
- self_query: bfloat16 [768, 768], P(('seq', 'shard')), may hold values from -0.0390625 to 0.0390625
- self_key: bfloat16 [768, 768], P(('seq', 'shard')), may hold values from -0.21875 to 0.21875
- self_value: bfloat16 [768, 768], P(('seq', 'shard')), may hold values from -0.21875 to 0.21875
- self_out: bfloat16 [768, 768], P(('seq', 'shard')), may hold values from -3 to 3
- cross_query: bfloat16 [768, 768], P(('seq', 'shard')), may hold values from -0.0390625 to 0.0390625
- cross_key: bfloat16 [768, 768], P(('seq', 'shard')), may hold values from -0.21875 to 0.21875
- cross_value: bfloat16 [768, 768], P(('seq', 'shard')), may hold values from -0.21875 to 0.21875
- cross_out: bfloat16 [768, 768], P(('seq', 'shard')), may hold values from -3 to 3
- ff_gate: bfloat16 [768, 2048], P(('seq', 'shard')), may hold values from -0.21875 to 0.21875
- ff_up: bfloat16 [768, 2048], P(('seq', 'shard')), may hold values from -0.21875 to 0.21875
- ff_down: bfloat16 [2048, 768], P(('seq', 'shard')), may hold values from -0.125 to 0.125
- norm_self: bfloat16 [768], P(('seq', 'shard')), may hold values from 0.25 to 1.75
- norm_cross: bfloat16 [768], P(('seq', 'shard')), may hold values from 0.25 to 1.75
- norm_ff: bfloat16 [768], P(('seq', 'shard')), may hold values from 0.25 to 1.75
- bias_table: bfloat16 [384], P(('seq', 'shard')), may hold values from -4 to 4
Outputs:
- hidden_out: bfloat16 [16, 1024, 768], P('shard', 'seq')
- grad_hidden: bfloat16 [16, 1024, 768], P('shard', 'seq')
- grad_encoded: bfloat16 [16, 1024, 768], P('shard', 'seq')
- grad_self_query: float32 [768, 768], P(('seq', 'shard'))
- grad_self_key: float32 [768, 768], P(('seq', 'shard'))
- grad_self_value: float32 [768, 768], P(('seq', 'shard'))
- grad_self_out: float32 [768, 768], P(('seq', 'shard'))
- grad_cross_query: float32 [768, 768], P(('seq', 'shard'))
- grad_cross_key: float32 [768, 768], P(('seq', 'shard'))
- grad_cross_value: float32 [768, 768], P(('seq', 'shard'))
- grad_cross_out: float32 [768, 768], P(('seq', 'shard'))
- grad_ff_gate: float32 [768, 2048], P(('seq', 'shard'))
- grad_ff_up: float32 [768, 2048], P(('seq', 'shard'))
- grad_ff_down: float32 [2048, 768], P(('seq', 'shard'))
- grad_norm_self: float32 [768], P(('seq', 'shard'))
- grad_norm_cross: float32 [768], P(('seq', 'shard'))
- grad_norm_ff: float32 [768], P(('seq', 'shard'))
- grad_bias_table: float32 [384], P(('seq', 'shard'))
Inputs may be any that keep to these rules, and one draw needn't show every extreme that they name: `buckets`: bucket of the distance d from a key to a later query, for d = 0 to 1023: never falling as d grows, equal to d for d below 16, and 31 at the largest distance.
All inputs are finite; a program needn't handle non-finite values.
Results may differ from a plain program's by a relative error of at most 0.024.
The roundings to bfloat16 on the way count: a program that leaves them out, or rounds other values in their place, can miss the bound.
Values may be sent and summed in bfloat16 or wider, within the bound.
A program may use at most 320 MiB of HBM per device.

v0:
```python
import jax
import jax.numpy as jnp
from jax import lax
from jax.sharding import PartitionSpec as P

H = 12
BUCKETS = 32


EPSILON = 1e-06
BLOCK = 512
NEGATIVE = -1e30


def dot_low(left, right):
    return jnp.dot(left, right, preferred_element_type=jnp.float32)


def dot_left(left, right):
    return lax.dot_general(
        left, right, (((0,), (0,)), ((), ())), preferred_element_type=jnp.float32
    )


def dot_right(left, right):
    return lax.dot_general(
        left, right, (((1,), (1,)), ((), ())), preferred_element_type=jnp.float32
    )


def rms_norm(value, gain):
    return value * lax.rsqrt(jnp.mean(value * value, -1, keepdims=True) + EPSILON) * gain


def norm_back(value, gain, grad):
    return jax.vjp(rms_norm, value, gain)[1](grad)


def gated(gate, upper):
    return jax.nn.gelu(gate, approximate=True) * upper


def row_blocks(rows):
    return [(start, min(BLOCK, rows - start)) for start in range(0, rows, BLOCK)]


def split_heads(value, heads):
    return value.reshape(value.shape[0], heads, -1)


def scores_of(queries, keys_all, start, bias_parts):
    scores = jnp.einsum("qhd,khd->hqk", queries, keys_all, preferred_element_type=jnp.float32)
    if bias_parts is None:
        return (scores, None)
    table_low, thresholds = bias_parts
    gap = (start + jnp.arange(queries.shape[0], dtype=jnp.int32))[:, None] - jnp.arange(
        keys_all.shape[0], dtype=jnp.int32
    )[None, :]
    places = jnp.maximum(gap, 0)
    reached = (places[:, :, None] >= thresholds[None, None, :]).astype(jnp.bfloat16)
    beyond = jnp.concatenate(
        [reached[:, :, 1:], jnp.zeros(reached.shape[:2] + (1,), jnp.bfloat16)], 2
    )
    bucket_hot = reached - beyond
    bias = jnp.einsum("qkb,hb->hqk", bucket_hot, table_low, preferred_element_type=jnp.float32)
    scores = jnp.where((gap >= 0)[None], scores + bias, NEGATIVE)
    return (scores, bucket_hot)


def attend(queries, keys_all, values, heads, bias_parts):
    query_heads = split_heads(queries, heads)
    key_heads = split_heads(keys_all, heads)
    value_heads = split_heads(values, heads)
    pieces = []
    stats = []
    for start, size in row_blocks(queries.shape[0]):
        finish = start + size if bias_parts is not None else key_heads.shape[0]
        scores, unused = scores_of(
            query_heads[start : start + size], key_heads[:finish], start, bias_parts
        )
        summit = jnp.max(scores, -1, keepdims=True)
        exponent = jnp.exp(scores - summit)
        total = jnp.sum(exponent, -1, keepdims=True)
        weights = (exponent / total).astype(jnp.bfloat16)
        mixed = jnp.einsum(
            "hqk,khd->qhd", weights, value_heads[:finish], preferred_element_type=jnp.float32
        )
        pieces.append(mixed.reshape(size, -1))
        stats.append(summit + jnp.log(total))
    return (jnp.concatenate(pieces, 0).astype(jnp.bfloat16), stats)


def attend_back(queries, keys_all, values, grad_mixed, stats, heads, bias_parts):
    query_heads = split_heads(queries, heads)
    key_heads = split_heads(keys_all, heads)
    value_heads = split_heads(values, heads)
    grad_heads = split_heads(grad_mixed, heads)
    count = key_heads.shape[0]
    grad_keys = jnp.zeros(key_heads.shape, jnp.float32)
    grad_values = jnp.zeros(value_heads.shape, jnp.float32)
    bucket_grad = jnp.zeros((heads, BUCKETS), jnp.float32)
    grad_queries = []
    for block, (start, size) in enumerate(row_blocks(queries.shape[0])):
        finish = start + size if bias_parts is not None else count
        block_query = query_heads[start : start + size]
        block_grad = grad_heads[start : start + size]
        scores, bucket_hot = scores_of(block_query, key_heads[:finish], start, bias_parts)
        probs = jnp.exp(scores - stats[block])
        grad_probs = jnp.einsum(
            "qhd,khd->hqk", block_grad, value_heads[:finish], preferred_element_type=jnp.float32
        )
        inner = jnp.sum(probs * grad_probs, -1, keepdims=True)
        grad_scores = (probs * (grad_probs - inner)).astype(jnp.bfloat16)
        grad_queries.append(
            jnp.einsum(
                "hqk,khd->qhd", grad_scores, key_heads[:finish], preferred_element_type=jnp.float32
            ).reshape(size, -1)
        )
        grad_keys = grad_keys.at[:finish].add(
            jnp.einsum("hqk,qhd->khd", grad_scores, block_query, preferred_element_type=jnp.float32)
        )
        grad_values = grad_values.at[:finish].add(
            jnp.einsum(
                "hqk,qhd->khd",
                probs.astype(jnp.bfloat16),
                block_grad,
                preferred_element_type=jnp.float32,
            )
        )
        if bias_parts is not None:
            bucket_grad = bucket_grad + jnp.einsum(
                "hqk,qkb->hb", grad_scores, bucket_hot, preferred_element_type=jnp.float32
            )
    return (
        jnp.concatenate(grad_queries, 0),
        grad_keys.reshape(count, -1),
        grad_values.reshape(count, -1),
        bucket_grad,
    )


def on_device(
    hidden_in,
    encoded,
    cotangent,
    buckets,
    self_query,
    self_key,
    self_value,
    self_out,
    cross_query,
    cross_key,
    cross_value,
    cross_out,
    ff_gate,
    ff_up,
    ff_down,
    norm_self,
    norm_cross,
    norm_ff,
    bias_table,
):
    (
        w_query,
        w_key,
        w_value,
        w_sout,
        w_cquery,
        w_ckey,
        w_cvalue,
        w_cout,
        w_gate,
        w_up,
        w_down,
        gain_one,
        gain_two,
        gain_three,
        table_all,
    ) = (
        lax.all_gather(self_query, ("seq", "shard"), axis=0, tiled=True),
        lax.all_gather(self_key, ("seq", "shard"), axis=0, tiled=True),
        lax.all_gather(self_value, ("seq", "shard"), axis=0, tiled=True),
        lax.all_gather(self_out, ("seq", "shard"), axis=0, tiled=True),
        lax.all_gather(cross_query, ("seq", "shard"), axis=0, tiled=True),
        lax.all_gather(cross_key, ("seq", "shard"), axis=0, tiled=True),
        lax.all_gather(cross_value, ("seq", "shard"), axis=0, tiled=True),
        lax.all_gather(cross_out, ("seq", "shard"), axis=0, tiled=True),
        lax.all_gather(ff_gate, ("seq", "shard"), axis=0, tiled=True),
        lax.all_gather(ff_up, ("seq", "shard"), axis=0, tiled=True),
        lax.all_gather(ff_down, ("seq", "shard"), axis=0, tiled=True),
        lax.all_gather(norm_self, ("seq", "shard"), axis=0, tiled=True),
        lax.all_gather(norm_cross, ("seq", "shard"), axis=0, tiled=True),
        lax.all_gather(norm_ff, ("seq", "shard"), axis=0, tiled=True),
        lax.all_gather(bias_table, ("seq", "shard"), axis=0, tiled=True),
    )
    seq_pos = lax.axis_index("seq")
    heads_local = H // lax.axis_size("seq")
    hidden = hidden_in[0].astype(jnp.float32)
    enc_rows = encoded[0]
    table_rows = lax.dynamic_slice_in_dim(
        table_all.reshape(H, BUCKETS), seq_pos * heads_local, heads_local, 0
    )
    thresholds = jnp.sum(
        (buckets[None, :] < jnp.arange(BUCKETS, dtype=jnp.int32)[:, None]).astype(jnp.int32), 1
    )
    bias_parts = (table_rows, thresholds)
    first = rms_norm(hidden, gain_one.astype(jnp.float32)).astype(jnp.bfloat16)
    packed = jnp.stack(
        [dot_low(first, w_query), dot_low(first, w_key), dot_low(first, w_value)]
    ).astype(jnp.bfloat16)
    spread = lax.all_to_all(packed, "seq", split_axis=2, concat_axis=1, tiled=True)
    self_mixed, self_stats = attend(spread[0], spread[1], spread[2], heads_local, bias_parts)
    self_back = lax.all_to_all(self_mixed, "seq", split_axis=0, concat_axis=1, tiled=True)
    after_self = hidden + dot_low(self_back, w_sout)
    second = rms_norm(after_self, gain_two.astype(jnp.float32)).astype(jnp.bfloat16)
    packed_cross = jnp.stack(
        [dot_low(second, w_cquery), dot_low(enc_rows, w_ckey), dot_low(enc_rows, w_cvalue)]
    ).astype(jnp.bfloat16)
    cross_spread = lax.all_to_all(packed_cross, "seq", split_axis=2, concat_axis=1, tiled=True)
    cross_mixed, cross_stats = attend(
        cross_spread[0], cross_spread[1], cross_spread[2], heads_local, None
    )
    cross_back = lax.all_to_all(cross_mixed, "seq", split_axis=0, concat_axis=1, tiled=True)
    after_cross = after_self + dot_low(cross_back, w_cout)
    third = rms_norm(after_cross, gain_three.astype(jnp.float32)).astype(jnp.bfloat16)
    gate = dot_low(third, w_gate)
    upper = dot_low(third, w_up)
    inner = gated(gate, upper).astype(jnp.bfloat16)
    hidden_out = (after_cross + dot_low(inner, w_down)).astype(jnp.bfloat16)
    (
        w_query,
        w_key,
        w_value,
        w_sout,
        w_cquery,
        w_ckey,
        w_cvalue,
        w_cout,
        w_gate,
        w_up,
        w_down,
        gain_one,
        gain_two,
        gain_three,
    ) = (
        lax.all_gather(self_query, ("seq", "shard"), axis=0, tiled=True),
        lax.all_gather(self_key, ("seq", "shard"), axis=0, tiled=True),
        lax.all_gather(self_value, ("seq", "shard"), axis=0, tiled=True),
        lax.all_gather(self_out, ("seq", "shard"), axis=0, tiled=True),
        lax.all_gather(cross_query, ("seq", "shard"), axis=0, tiled=True),
        lax.all_gather(cross_key, ("seq", "shard"), axis=0, tiled=True),
        lax.all_gather(cross_value, ("seq", "shard"), axis=0, tiled=True),
        lax.all_gather(cross_out, ("seq", "shard"), axis=0, tiled=True),
        lax.all_gather(ff_gate, ("seq", "shard"), axis=0, tiled=True),
        lax.all_gather(ff_up, ("seq", "shard"), axis=0, tiled=True),
        lax.all_gather(ff_down, ("seq", "shard"), axis=0, tiled=True),
        lax.all_gather(norm_self, ("seq", "shard"), axis=0, tiled=True),
        lax.all_gather(norm_cross, ("seq", "shard"), axis=0, tiled=True),
        lax.all_gather(norm_ff, ("seq", "shard"), axis=0, tiled=True),
    )
    grad_top = cotangent[0]
    grad_wdown = dot_left(inner, grad_top)
    grad_inner = dot_right(grad_top, w_down)
    grad_gate, grad_upper = jax.vjp(gated, gate, upper)[1](grad_inner)
    gate_low = grad_gate.astype(jnp.bfloat16)
    upper_low = grad_upper.astype(jnp.bfloat16)
    grad_wgate = dot_left(third, gate_low)
    grad_wup = dot_left(third, upper_low)
    grad_third = dot_right(gate_low, w_gate) + dot_right(upper_low, w_up)
    norm_grad, grad_gain_three = norm_back(after_cross, gain_three.astype(jnp.float32), grad_third)
    grad_cross_res = grad_top.astype(jnp.float32) + norm_grad
    cross_res_low = grad_cross_res.astype(jnp.bfloat16)
    grad_wcout = dot_left(cross_back, cross_res_low)
    grad_cross_mix = dot_right(cross_res_low, w_cout).astype(jnp.bfloat16)
    grad_spread = lax.all_to_all(grad_cross_mix, "seq", split_axis=1, concat_axis=0, tiled=True)
    cross_parts = attend_back(
        cross_spread[0],
        cross_spread[1],
        cross_spread[2],
        grad_spread,
        cross_stats,
        heads_local,
        None,
    )
    packed_back = jnp.stack([cross_parts[0], cross_parts[1], cross_parts[2]]).astype(jnp.bfloat16)
    cross_grads = lax.all_to_all(packed_back, "seq", split_axis=1, concat_axis=2, tiled=True)
    grad_cq = cross_grads[0]
    grad_ck = cross_grads[1]
    grad_cv = cross_grads[2]
    grad_wcquery = dot_left(second, grad_cq)
    grad_wckey = dot_left(enc_rows, grad_ck)
    grad_wcvalue = dot_left(enc_rows, grad_cv)
    grad_encoded = (dot_right(grad_ck, w_ckey) + dot_right(grad_cv, w_cvalue)).astype(jnp.bfloat16)
    norm_grad, grad_gain_two = norm_back(
        after_self, gain_two.astype(jnp.float32), dot_right(grad_cq, w_cquery)
    )
    grad_self_res = grad_cross_res + norm_grad
    self_res_low = grad_self_res.astype(jnp.bfloat16)
    grad_wsout = dot_left(self_back, self_res_low)
    grad_self_mix = dot_right(self_res_low, w_sout).astype(jnp.bfloat16)
    grad_self_spread = lax.all_to_all(grad_self_mix, "seq", split_axis=1, concat_axis=0, tiled=True)
    self_parts = attend_back(
        spread[0], spread[1], spread[2], grad_self_spread, self_stats, heads_local, bias_parts
    )
    packed_self = jnp.stack([self_parts[0], self_parts[1], self_parts[2]]).astype(jnp.bfloat16)
    self_grads = lax.all_to_all(packed_self, "seq", split_axis=1, concat_axis=2, tiled=True)
    grad_wquery = dot_left(first, self_grads[0])
    grad_wkey = dot_left(first, self_grads[1])
    grad_wvalue = dot_left(first, self_grads[2])
    grad_first = (
        dot_right(self_grads[0], w_query)
        + dot_right(self_grads[1], w_key)
        + dot_right(self_grads[2], w_value)
    )
    norm_grad, grad_gain_one = norm_back(hidden, gain_one.astype(jnp.float32), grad_first)
    grad_hidden = (grad_self_res + norm_grad).astype(jnp.bfloat16)
    table_grad = lax.dynamic_update_slice_in_dim(
        jnp.zeros((H, BUCKETS), jnp.float32), self_parts[3], seq_pos * heads_local, 0
    ).reshape(-1)
    summed = (
        lax.psum_scatter(grad_wquery, ("seq", "shard"), scatter_dimension=0, tiled=True),
        lax.psum_scatter(grad_wkey, ("seq", "shard"), scatter_dimension=0, tiled=True),
        lax.psum_scatter(grad_wvalue, ("seq", "shard"), scatter_dimension=0, tiled=True),
        lax.psum_scatter(grad_wsout, ("seq", "shard"), scatter_dimension=0, tiled=True),
        lax.psum_scatter(grad_wcquery, ("seq", "shard"), scatter_dimension=0, tiled=True),
        lax.psum_scatter(grad_wckey, ("seq", "shard"), scatter_dimension=0, tiled=True),
        lax.psum_scatter(grad_wcvalue, ("seq", "shard"), scatter_dimension=0, tiled=True),
        lax.psum_scatter(grad_wcout, ("seq", "shard"), scatter_dimension=0, tiled=True),
        lax.psum_scatter(grad_wgate, ("seq", "shard"), scatter_dimension=0, tiled=True),
        lax.psum_scatter(grad_wup, ("seq", "shard"), scatter_dimension=0, tiled=True),
        lax.psum_scatter(grad_wdown, ("seq", "shard"), scatter_dimension=0, tiled=True),
        lax.psum_scatter(grad_gain_one, ("seq", "shard"), scatter_dimension=0, tiled=True),
        lax.psum_scatter(grad_gain_two, ("seq", "shard"), scatter_dimension=0, tiled=True),
        lax.psum_scatter(grad_gain_three, ("seq", "shard"), scatter_dimension=0, tiled=True),
        lax.psum_scatter(table_grad, ("seq", "shard"), scatter_dimension=0, tiled=True),
    )
    return (
        hidden_out[None],
        grad_hidden[None],
        grad_encoded[None],
        summed[0],
        summed[1],
        summed[2],
        summed[3],
        summed[4],
        summed[5],
        summed[6],
        summed[7],
        summed[8],
        summed[9],
        summed[10],
        summed[11],
        summed[12],
        summed[13],
        summed[14],
    )


def solution(mesh):
    placed = (
        P("shard", "seq", None),
        P("shard", "seq", None),
        P("shard", "seq", None),
        P(),
        P(("seq", "shard"), None),
        P(("seq", "shard"), None),
        P(("seq", "shard"), None),
        P(("seq", "shard"), None),
        P(("seq", "shard"), None),
        P(("seq", "shard"), None),
        P(("seq", "shard"), None),
        P(("seq", "shard"), None),
        P(("seq", "shard"), None),
        P(("seq", "shard"), None),
        P(("seq", "shard"), None),
        P(("seq", "shard")),
        P(("seq", "shard")),
        P(("seq", "shard")),
        P(("seq", "shard")),
    )
    return jax.shard_map(
        on_device,
        mesh=mesh,
        in_specs=placed,
        out_specs=(
            P("shard", "seq", None),
            P("shard", "seq", None),
            P("shard", "seq", None),
            P(("seq", "shard"), None),
            P(("seq", "shard"), None),
            P(("seq", "shard"), None),
            P(("seq", "shard"), None),
            P(("seq", "shard"), None),
            P(("seq", "shard"), None),
            P(("seq", "shard"), None),
            P(("seq", "shard"), None),
            P(("seq", "shard"), None),
            P(("seq", "shard"), None),
            P(("seq", "shard"), None),
            P(("seq", "shard")),
            P(("seq", "shard")),
            P(("seq", "shard")),
            P(("seq", "shard")),
        ),
        check_vma=False,
    )
```

profile of v0, /device:TPU:0, one launch (start us, length us, event | category | flops | bytes accessed | tf_op | source)
XLA Modules:
  0.0 1898.2 jit_solution(3791997634486352360)
XLA Ops:
  18.6 42.6 %all-reduce.14 = (bf16[768]{0:T(1024)(128)(2,1)S(1)}, bf16[12,32]{1,0:T(8,128)(2,1)S(1)}, bf16[768]{0:T(1024)(128)(2,1)S(1)}, bf16[768]{0:T(1024)(128)(2,1)}) all-reduce(bf16[768]{0:T(1024)(128)(2,1)S(1)} %dynamic-update-slice.18, bf16[12,32]{1,0:T(8,128)(2,1)S(1)} %reshape.626, ...), channel_id=1, replica_groups=mesh['seq'=2,'shard'=16] {'seq','shard'}, use_global_device_ids=true, to_apply=%add.4 | all-reduce | flops 2688 | bytes 10752
  89.1 30.7 %copy.238 = bf16[512,512,32]{1,2,0:T(8,128)(2,1)} copy(bf16[512,512,32]{0,2,1:T(8,128)(2,1)} %pad_subtract_fusion.1) | data formatting | bytes 33554432 | tf_op jit(solution)/shard_map/sub | solution.py:64
  152.9 22.8 %slice.329 = bf16[512,1024,31]{0,2,1:T(8,128)(2,1)} slice(bf16[512,1024,32]{0,2,1:T(8,128)(2,1)} %compare_convert_fusion), slice={[0:512], [0:1024], [1:32]} | slice | bytes 65011712 | tf_op jit(solution)/shard_map/slice | solution.py:62
  175.7 24.0 %pad_subtract_fusion = bf16[512,1024,32]{0,2,1:T(8,128)(2,1)} fusion(bf16[512,1024,31]{0,2,1:T(8,128)(2,1)} %slice.329, s32[32]{0:T(128)S(1)} %convert_reduce_fusion, s32[512,1024]{0,1:T(8,128)} %copy.243), kind=kLoop, calls=%fused_computation.1 | loop fusion | flops 100663296 | bytes 68157568 | tf_op jit(solution)/shard_map/sub | solution.py:64
  199.7 50.9 %copy.244 = bf16[512,1024,32]{1,2,0:T(8,128)(2,1)} copy(bf16[512,1024,32]{0,2,1:T(8,128)(2,1)} %pad_subtract_fusion) | data formatting | bytes 67108864 | tf_op jit(solution)/shard_map/sub | solution.py:64
  270.1 19.4 %fusion.98 = f32[6,512,1024]{2,0,1:T(8,128)} fusion(bf16[512,1024,32]{1,2,0:T(8,128)(2,1)} %copy.244, bf16[12,32]{1,0:T(8,128)(2,1)S(1)} %get-tuple-element.281, s32[]{:T(128)S(6)} %select_n.14), kind=kOutput, calls=%fused_computation.172 | convolution fusion | flops 201326592 | bytes 46139396 | tf_op jit(solution)/shard_map/qkb,hb->hqk/dot_general | solution.py:65
  289.5 19.9 %all-to-all-done = bf16[3,512,768]{1,0,2:T(4,128)(2,1)} async-done(((bf16[3,512,768]{1,0,2:T(4,128)(2,1)}), bf16[3,512,768]{1,0,2:T(4,128)(2,1)}, u32[]{:S(2)}, u32[]{:S(2)}) %all-to-all-start) | async-done | bytes 2359328 | tf_op jit(solution)/shard_map/all_to_all | solution.py:211
  335.4 14.9 fusion.127
  378.0 26.0 %all-gather.20.cloned.1.call-done = bf16[768,768]{1,0:T(8,128)(2,1)} async-done(((bf16[24,768]{1,0:T(8,128)(2,1)}), bf16[768,768]{1,0:T(8,128)(2,1)}) %all-gather.20.cloned.1.call-update) | async-done | bytes 1179664 | tf_op jit(solution)/shard_map/all_gather | solution.py:184
  419.8 39.2 %all-to-all-done.2 = bf16[3,512,768]{1,0,2:T(4,128)(2,1)} async-done(((bf16[3,512,768]{1,0,2:T(4,128)(2,1)}), bf16[3,512,768]{1,0,2:T(4,128)(2,1)}, u32[]{:S(2)}, u32[]{:S(2)}) %all-to-all-start.2) | async-done | bytes 2359328 | tf_op jit(solution)/shard_map/all_to_all | solution.py:219
  534.6 53.3 %all-gather.28.cloned.1.call-done = bf16[768,2048]{1,0:T(8,128)(2,1)} async-done(((bf16[24,2048]{1,0:T(8,128)(2,1)}), bf16[768,2048]{1,0:T(8,128)(2,1)}) %all-gather.28.cloned.1.call-update) | async-done | bytes 3145744 | tf_op jit(solution)/shard_map/all_gather | solution.py:188
  593.6 55.2 %all-gather.32.cloned.1.call-done = bf16[2048,768]{1,0:T(8,128)(2,1)} async-done(((bf16[64,768]{1,0:T(8,128)(2,1)}), bf16[2048,768]{1,0:T(8,128)(2,1)}) %all-gather.32.cloned.1.call-update) | async-done | bytes 3145744 | tf_op jit(solution)/shard_map/all_gather | solution.py:190
  759.0 38.8 %all_to_all.124 = bf16[3,1024,384]{2,0,1:T(4,128)(2,1)S(1)} all-to-all(bf16[3,1024,384]{2,0,1:T(4,128)(2,1)S(1)} %copy.263), channel_id=1, replica_groups=mesh['seq'=2,'shard'=16] {'seq'}, dimensions={1} | all-to-all | bytes 4718592 | tf_op jit(solution)/shard_map/all_to_all | solution.py:286
  898.8 36.6 %all_to_all.125 = bf16[3,1024,384]{2,0,1:T(4,128)(2,1)S(1)} all-to-all(bf16[3,1024,384]{2,0,1:T(4,128)(2,1)S(1)} %copy.276), channel_id=1, replica_groups=mesh['seq'=2,'shard'=16] {'seq'}, dimensions={1} | all-to-all | bytes 4718592 | tf_op jit(solution)/shard_map/all_to_all | solution.py:306
  989.3 16.3 convolution_bitcast_fusion.3
  1024.0 39.1 %all-reduce.13 = (f32[768]{0:T(1024)S(1)}, f32[768]{0:T(1024)S(1)}, f32[768]{0:T(1024)S(1)}, f32[384]{0:T(512)S(1)}) all-reduce(f32[768]{0:T(1024)S(1)} %get-tuple-element.274, f32[768]{0:T(1024)S(1)} %copy-done.91, f32[768]{0:T(1024)S(1)} %copy-done.90, f32[384]{0:T(512)S(1)} %reshape.635), channel_id=13, replica_groups=mesh['seq'=2,'shard'=16] {'seq','shard'}, use_global_device_ids=true, to_apply=%region_31.32.clone | all-reduce | flops 2688 | bytes 21504
  1068.3 44.6 %reduce-scatter.36.cloned.1.call-done = f32[24,768]{1,0:T(8,128)} async-done(((f32[768,768]{1,0:T(8,128)}), f32[24,768]{1,0:T(8,128)}) %reduce-scatter.36.cloned.1.call-update) | async-done | bytes 73744
  1112.9 104.4 %reduce-scatter.34.cloned.1.call-done = f32[24,768]{1,0:T(8,128)} async-done(((f32[768,768]{1,0:T(8,128)}), f32[24,768]{1,0:T(8,128)}) %reduce-scatter.34.cloned.1.call-update) | async-done | bytes 73744
  1217.3 104.4 %reduce-scatter.20.cloned.1.call-done = f32[24,768]{1,0:T(8,128)} async-done(((f32[768,768]{1,0:T(8,128)}), f32[24,768]{1,0:T(8,128)}) %reduce-scatter.20.cloned.1.call-update) | async-done | bytes 73744 | tf_op jit(solution)/shard_map/reduce_scatter | solution.py:323
  1321.8 104.4 %reduce-scatter.16.cloned.1.call-done = f32[24,768]{1,0:T(8,128)} async-done(((f32[768,768]{1,0:T(8,128)}), f32[24,768]{1,0:T(8,128)}) %reduce-scatter.16.cloned.1.call-update) | async-done | bytes 73744 | tf_op jit(solution)/shard_map/reduce_scatter | solution.py:321
  1426.2 104.5 %reduce-scatter.18.cloned.1.call-done = f32[24,768]{1,0:T(8,128)} async-done(((f32[768,768]{1,0:T(8,128)}), f32[24,768]{1,0:T(8,128)}) %reduce-scatter.18.cloned.1.call-update) | async-done | bytes 73744 | tf_op jit(solution)/shard_map/reduce_scatter | solution.py:322
  1530.7 120.0 %reduce-scatter.32.cloned.1.call-done = f32[64,768]{1,0:T(8,128)} async-done(((f32[2048,768]{1,0:T(8,128)}), f32[64,768]{1,0:T(8,128)}) %reduce-scatter.32.cloned.1.call-update) | async-done | bytes 196624 | tf_op jit(solution)/shard_map/reduce_scatter | solution.py:331
  1650.7 120.2 %reduce-scatter.30.cloned.1.call-done = f32[24,2048]{1,0:T(8,128)} async-done(((f32[768,2048]{1,0:T(8,128)}), f32[24,2048]{1,0:T(8,128)}) %reduce-scatter.30.cloned.1.call-update) | async-done | bytes 196624 | tf_op jit(solution)/shard_map/reduce_scatter | solution.py:330
  1771.0 120.2 %reduce-scatter.28.cloned.1.call-done = f32[24,2048]{1,0:T(8,128)} async-done(((f32[768,2048]{1,0:T(8,128)}), f32[24,2048]{1,0:T(8,128)}) %reduce-scatter.28.cloned.1.call-update) | async-done | bytes 196624 | tf_op jit(solution)/shard_map/reduce_scatter | solution.py:329
  (461 shorter events, 529.5 us)
Async XLA Ops:
  7.2 243.4 %all-gather.14.cloned.1.call-start = ((), (), s32[]{:S(2)}) async-start(), calls=%async_computation.20 | async-start | bytes 1216512 | tf_op jit(solution)/shard_map/all_gather | solution.py:181
  8.0 244.8 %all-gather.16.cloned.1.call-start = ((), (), s32[]{:S(2)}) async-start(), calls=%async_computation.21 | async-start | bytes 1216512 | tf_op jit(solution)/shard_map/all_gather | solution.py:182
  8.7 246.2 %all-gather.12.cloned.1.call-start = ((), (), s32[]{:S(2)}) async-start(), calls=%async_computation.19 | async-start | bytes 1216512 | tf_op jit(solution)/shard_map/all_gather | solution.py:180
  9.4 353.7 %all-gather.24.cloned.1.call-start = ((), (), s32[]{:S(2)}) async-start(), calls=%async_computation.25 | async-start | bytes 1216512 | tf_op jit(solution)/shard_map/all_gather | solution.py:186
  10.0 356.1 %all-gather.22.cloned.1.call-start = ((), (), s32[]{:S(2)}) async-start(), calls=%async_computation.24 | async-start | bytes 1216512 | tf_op jit(solution)/shard_map/all_gather | solution.py:185
  10.6 364.4 %all-gather.18.cloned.1.call-start = ((), (), s32[]{:S(2)}) async-start(), calls=%async_computation.22 | async-start | bytes 1216512 | tf_op jit(solution)/shard_map/all_gather | solution.py:183
  11.2 392.9 %all-gather.20.cloned.1.call-start = ((), (), s32[]{:S(2)}) async-start(), calls=%async_computation.23 | async-start | bytes 1216512 | tf_op jit(solution)/shard_map/all_gather | solution.py:184
  11.9 512.8 %all-gather.26.cloned.1.call-start = ((), (), s32[]{:S(2)}) async-start(), calls=%async_computation.26 | async-start | bytes 1216512 | tf_op jit(solution)/shard_map/all_gather | solution.py:187
  12.7 516.0 %all-gather.30.cloned.1.call-start = ((), (), s32[]{:S(2)}) async-start(), calls=%async_computation.28 | async-start | bytes 3244032 | tf_op jit(solution)/shard_map/all_gather | solution.py:189
  13.4 574.5 %all-gather.28.cloned.1.call-start = ((), (), s32[]{:S(2)}) async-start(), calls=%async_computation.27 | async-start | bytes 3244032 | tf_op jit(solution)/shard_map/all_gather | solution.py:188
  264.9 44.5 %all-to-all-start = ((bf16[3,512,768]{1,0,2:T(4,128)(2,1)}), bf16[3,512,768]{1,0,2:T(4,128)(2,1)}, u32[]{:S(2)}, u32[]{:S(2)}) async-start(bf16[3,512,768]{1,0,2:T(4,128)(2,1)} %copy.236), calls=%async_computation | async-start | bytes 6291456 | tf_op jit(solution)/shard_map/all_to_all | solution.py:211
  413.9 45.2 %all-to-all-start.2 = ((bf16[3,512,768]{1,0,2:T(4,128)(2,1)}), bf16[3,512,768]{1,0,2:T(4,128)(2,1)}, u32[]{:S(2)}, u32[]{:S(2)}) async-start(bf16[3,512,768]{1,0,2:T(4,128)(2,1)} %copy.249), calls=%async_computation.2 | async-start | bytes 6291456 | tf_op jit(solution)/shard_map/all_to_all | solution.py:219
  419.1 229.6 %all-gather.32.cloned.1.call-start = ((), (), s32[]{:S(2)}) async-start(), calls=%async_computation.29 | async-start | bytes 3244032 | tf_op jit(solution)/shard_map/all_gather | solution.py:190
  671.3 396.9 %reduce-scatter.26.cloned.1.call-start = ((), (), s32[]{:S(2)}) async-start(), calls=%async_computation.35 | async-start | bytes 2433024 | tf_op jit(solution)/shard_map/reduce_scatter | solution.py:328
  675.5 392.8 %reduce-scatter.24.cloned.1.call-start = ((), (), s32[]{:S(2)}) async-start(), calls=%async_computation.34 | async-start | bytes 2433024 | tf_op jit(solution)/shard_map/reduce_scatter | solution.py:325
  805.4 262.9 %reduce-scatter.22.cloned.1.call-start = ((), (), s32[]{:S(2)}) async-start(), calls=%async_computation.33 | async-start | bytes 2433024 | tf_op jit(solution)/shard_map/reduce_scatter | solution.py:324
  812.6 300.3 %reduce-scatter.36.cloned.1.call-start = ((), (), s32[]{:S(2)}) async-start(), calls=%async_computation.40 | async-start | bytes 2433024
  826.8 390.5 %reduce-scatter.34.cloned.1.call-start = ((), (), s32[]{:S(2)}) async-start(), calls=%async_computation.39 | async-start | bytes 2433024
  832.1 489.7 %reduce-scatter.20.cloned.1.call-start = ((), (), s32[]{:S(2)}) async-start(), calls=%async_computation.32 | async-start | bytes 2433024 | tf_op jit(solution)/shard_map/reduce_scatter | solution.py:323
  941.0 485.2 %reduce-scatter.16.cloned.1.call-start = ((), (), s32[]{:S(2)}) async-start(), calls=%async_computation.30 | async-start | bytes 2433024 | tf_op jit(solution)/shard_map/reduce_scatter | solution.py:321
  944.9 585.8 %reduce-scatter.18.cloned.1.call-start = ((), (), s32[]{:S(2)}) async-start(), calls=%async_computation.31 | async-start | bytes 2433024 | tf_op jit(solution)/shard_map/reduce_scatter | solution.py:322
  947.7 703.0 %reduce-scatter.32.cloned.1.call-start = ((), (), s32[]{:S(2)}) async-start(), calls=%async_computation.38 | async-start | bytes 6488064 | tf_op jit(solution)/shard_map/reduce_scatter | solution.py:331
  953.8 817.1 %reduce-scatter.30.cloned.1.call-start = ((), (), s32[]{:S(2)}) async-start(), calls=%async_computation.37 | async-start | bytes 6488064 | tf_op jit(solution)/shard_map/reduce_scatter | solution.py:330
  961.0 930.1 %reduce-scatter.28.cloned.1.call-start = ((), (), s32[]{:S(2)}) async-start(), calls=%async_computation.36 | async-start | bytes 6488064 | tf_op jit(solution)/shard_map/reduce_scatter | solution.py:329
  (114 other events, 1895.7 us)
Sparse Core Ops, SparseCore 0:
  10.9 56.8 all-gather.13
  70.7 53.1 all-gather.15
  126.8 52.8 all-gather.11
  182.5 52.8 all-gather.23
  238.2 54.2 all-gather.21
  295.2 52.9 all-gather.17
  351.1 52.9 all-gather.19
  406.9 54.9 all-gather.25
  464.9 62.3 all-gather.29
  530.0 57.8 all-gather.27
  590.8 57.8 all-gather.31
  677.7 99.9 reduce-scatter.25
  805.5 98.5 reduce-scatter.23
  909.8 98.6 reduce-scatter.21
  1014.2 98.6 reduce-scatter.35
  1118.6 98.6 reduce-scatter.33
  1223.0 98.6 reduce-scatter.19
  1327.5 98.6 reduce-scatter.15
  1432.0 98.6 reduce-scatter.17
  1536.8 113.8 reduce-scatter.31
  1656.9 113.9 reduce-scatter.29
  1777.2 113.9 reduce-scatter.27
where the time goes:
time: 1910 us; the launch traced here: 1900 us
  waiting for transfers between devices  1050 us (55%)
  matrix products  283 us (15%)
  local copies, waits for them, and re-layouts  246 us (13%)
  blocking collectives  157 us (8%)
  other arithmetic  114 us (6%)
  starting transfers between devices  28.6 us (1%)
    unnamed x24, waiting for transfers between devices  156 us
    reduce_scatter x1, waiting for transfers between devices, on_device(): lax.psum_scatter(grad_wup, ('seq', 'shard'), scatter_dimension=0, tiled=T...  120 us
    reduce_scatter x1, waiting for transfers between devices, on_device(): lax.psum_scatter(grad_wgate, ('seq', 'shard'), scatter_dimension=0, tiled...  120 us
    reduce_scatter x1, waiting for transfers between devices, on_device(): lax.psum_scatter(grad_wdown, ('seq', 'shard'), scatter_dimension=0, tiled...  120 us
    reduce_scatter x1, waiting for transfers between devices, on_device(): lax.psum_scatter(grad_wkey, ('seq', 'shard'), scatter_dimension=0, tiled=...  105 us
    reduce_scatter x1, waiting for transfers between devices, on_device(): lax.psum_scatter(grad_wquery, ('seq', 'shard'), scatter_dimension=0, tile...  104 us
    reduce_scatter x1, waiting for transfers between devices, on_device(): lax.psum_scatter(grad_wvalue, ('seq', 'shard'), scatter_dimension=0, tile...  104 us
    unnamed x2, blocking collectives  81.7 us
  transfers between devices with their start and end apart: 28, of which 17 were waited for; matrix products, arithmetic and copies ran while one was open for 32% of the time, Pallas kernels for 0%

commit v1 on v0

v1 whole, which is shorter than its diff:
```python
import functools
import jax
import jax.numpy as jnp
from jax import lax
from jax.experimental import pallas as pl
from jax.experimental.pallas import tpu as pltpu
from jax.sharding import PartitionSpec as P

H = 12
BUCKETS = 32
NEGATIVE = -1e30
EPSILON = 1e-06
F32 = jnp.float32
LOW = jnp.bfloat16
PAIR = 2
TILE = 256


def contract(left, right, left_dim, right_dim):
    return lax.dot_general(
        left, right, (((left_dim,), (right_dim,)), ((), ())), preferred_element_type=F32
    )


def keep_head(value, head):
    size = value.shape[1] // PAIR
    lane = lax.broadcasted_iota(jnp.int32, value.shape, 1)
    inside = (lane >= head * size) & (lane < (head + 1) * size)
    return jnp.where(inside, value, jnp.zeros_like(value))


def toeplitz(row):
    wide = jnp.broadcast_to(row, (TILE, 2 * TILE))
    return pltpu.roll(wide, 0, 1, stride=1, stride_axis=0)[:, :TILE]


def skew_sum(total_ref):
    group = 8
    width = 2 * TILE
    summed = jnp.zeros((group, width), F32)
    for start in range(0, TILE, group):
        rows = total_ref[start : start + group, :]
        wide = jnp.concatenate([rows, jnp.zeros_like(rows)], 1)
        summed = summed + pltpu.roll(wide, (width - start) % width, 1)
    out = summed[0:1]
    for row in range(1, group):
        out = out + pltpu.roll(summed[row : row + 1], width - row, 1)
    return out


def scores_t(keys, query, tiles, last):
    scores = contract(keys, query, 1, 1)
    if tiles is None:
        return scores
    parts = [
        scores[place * TILE : (place + 1) * TILE] + tiles[last - place] for place in range(last + 1)
    ]
    return jnp.concatenate(parts, 0) if len(parts) > 1 else parts[0]


def attend_block(q_ref, k_ref, v_t, o_ref, lse_ref, tiles_ref, start, last, span):
    query = q_ref[start : start + TILE, :]
    size = query.shape[1] // PAIR
    mixed = []
    for head in range(PAIR):
        tiles = None if tiles_ref is None else tiles_ref.at[head]
        scores = scores_t(k_ref[:span, :], keep_head(query, head), tiles, last)
        summit = jnp.max(scores, 0, keepdims=True)
        exponent = jnp.exp(scores - summit)
        total = jnp.sum(exponent, 0, keepdims=True)
        weighted = contract(
            v_t[head * size : (head + 1) * size, :span], exponent.astype(LOW), 1, 0
        )
        mixed.append(weighted / total)
        lse_ref[0, head : head + 1, start : start + TILE] = summit + jnp.log(total)
    o_ref[start : start + TILE, :] = jnp.concatenate(mixed, 0).T.astype(LOW)


def attend_kernel(causal, *refs):
    if causal:
        seq_ref, q_ref, k_ref, v_ref, z_ref, o_ref, lse_ref, tiles_ref = refs
        make_tiles(z_ref, tiles_ref)
    else:
        q_ref, k_ref, v_ref, o_ref, lse_ref = refs
    v_t = v_ref[...].T
    blocks = q_ref.shape[0] // TILE
    keys = k_ref.shape[0]
    if not causal:
        for block in range(blocks):
            attend_block(q_ref, k_ref, v_t, o_ref, lse_ref, None, block * TILE, None, keys)
        return
    for side in range(keys // q_ref.shape[0]):

        @pl.when(seq_ref[0] == side)
        def _(side=side):
            for block in range(blocks):
                last = side * blocks + block
                attend_block(
                    q_ref, k_ref, v_t, o_ref, lse_ref, tiles_ref, block * TILE, last,
                    (last + 1) * TILE,
                )


def make_tiles(z_ref, tiles_ref):
    for head in range(PAIR):
        for off in range(z_ref.shape[2]):
            tiles_ref[head, off] = toeplitz(z_ref[0, head, off : off + 1, :])


def attend(queries, keys_all, values, seq_pos, rows):
    count, width = queries.shape
    length = keys_all.shape[0]
    pairs = H // PAIR
    lanes = width // pairs
    offs = length // TILE
    causal = rows is not None
    col = lambda size: pl.BlockSpec((size, lanes), lambda pair, *_: (0, pair))
    in_specs = [col(count), col(length), col(length)]
    args = [queries, keys_all, values]
    scratch = []
    if causal:
        in_specs.append(pl.BlockSpec((1, PAIR, offs, 2 * TILE), lambda pair, *_: (pair, 0, 0, 0)))
        args = [seq_pos] + args + [rows]
        scratch = [pltpu.VMEM((PAIR, offs, TILE, TILE), F32)]
    work = H * count * length
    return pl.pallas_call(
        functools.partial(attend_kernel, causal),
        grid_spec=pltpu.PrefetchScalarGridSpec(
            num_scalar_prefetch=1 if causal else 0,
            grid=(pairs,),
            in_specs=in_specs,
            out_specs=[
                col(count),
                pl.BlockSpec((1, PAIR, count), lambda pair, *_: (pair, 0, 0)),
            ],
            scratch_shapes=scratch,
        ),
        out_shape=[
            jax.ShapeDtypeStruct((count, width), LOW),
            jax.ShapeDtypeStruct((pairs, PAIR, count), F32),
        ],
        cost_estimate=pl.CostEstimate(
            flops=work * 256 * 2, bytes_accessed=6 * length * width, transcendentals=work
        ),
        name="attend_causal" if causal else "attend_cross",
    )(*args)


def back_block(refs, k_t, prod_t, start, last, span, first, tiles_ref, total_ref):
    q_ref, k_ref, v_ref, g_ref, lse_ref, dq_ref, dk_acc, dv_acc = refs
    query = q_ref[start : start + TILE, :]
    grad = g_ref[start : start + TILE, :]
    size = query.shape[1] // PAIR
    dq_t = []
    dk = dv = None
    for head in range(PAIR):
        own = keep_head(query, head)
        own_grad = keep_head(grad, head)
        tiles = None if tiles_ref is None else tiles_ref.at[head]
        scores = scores_t(k_ref[:span, :], own, tiles, last)
        probs = jnp.exp(scores - lse_ref[0, head : head + 1, start : start + TILE])
        grad_probs = contract(v_ref[:span, :], own_grad, 1, 1)
        delta = jnp.sum(
            prod_t[head * size : (head + 1) * size, start : start + TILE], 0, keepdims=True
        )
        grad_scores = probs * (grad_probs - delta)
        low = grad_scores.astype(LOW)
        dv_new = contract(probs.astype(LOW), own_grad, 1, 0)
        dk_new = contract(low, own, 1, 0)
        dv = dv_new if dv is None else dv + dv_new
        dk = dk_new if dk is None else dk + dk_new
        dq_t.append(contract(k_t[head * size : (head + 1) * size, :span], low, 1, 0))
        if total_ref is not None:
            for place in range(last + 1):
                off = last - place
                piece = grad_scores[place * TILE : (place + 1) * TILE]
                if first:
                    total_ref[head, off] = piece
                elif off == last:
                    total_ref[head, off] = piece
                else:
                    total_ref[head, off] += piece
    dq_ref[start : start + TILE, :] = jnp.concatenate(dq_t, 0).T.astype(LOW)
    if first:
        dk_acc[:span, :] = dk
        dv_acc[:span, :] = dv
        if span < dk_acc.shape[0]:
            dk_acc[span:, :] = jnp.zeros((dk_acc.shape[0] - span, dk_acc.shape[1]), F32)
            dv_acc[span:, :] = jnp.zeros((dv_acc.shape[0] - span, dv_acc.shape[1]), F32)
    else:
        dk_acc[:span, :] += dk
        dv_acc[:span, :] += dv


def back_kernel(causal, *refs):
    if causal:
        (seq_ref, q_ref, k_ref, v_ref, g_ref, o_ref, lse_ref, z_ref,
         dq_ref, dk_ref, dv_ref, row_ref, dk_acc, dv_acc, tiles_ref, total_ref) = refs
        make_tiles(z_ref, tiles_ref)
    else:
        (q_ref, k_ref, v_ref, g_ref, o_ref, lse_ref,
         dq_ref, dk_ref, dv_ref, dk_acc, dv_acc) = refs
        tiles_ref = total_ref = None
    k_t = k_ref[...].T
    prod_t = (g_ref[...].astype(F32) * o_ref[...].astype(F32)).T
    blocks = q_ref.shape[0] // TILE
    keys = k_ref.shape[0]
    main = (q_ref, k_ref, v_ref, g_ref, lse_ref, dq_ref, dk_acc, dv_acc)
    if not causal:
        for block in range(blocks):
            back_block(main, k_t, prod_t, block * TILE, None, keys, block == 0, None, None)
    else:
        for side in range(keys // q_ref.shape[0]):

            @pl.when(seq_ref[0] == side)
            def _(side=side):
                for block in range(blocks):
                    last = side * blocks + block
                    back_block(
                        main, k_t, prod_t, block * TILE, last, (last + 1) * TILE,
                        block == 0, tiles_ref, total_ref,
                    )
                for head in range(PAIR):
                    for off in range(keys // TILE):
                        if off < (side + 1) * blocks:
                            row_ref[0, head, off : off + 1, :] = skew_sum(total_ref.at[head, off])
                        else:
                            row_ref[0, head, off : off + 1, :] = jnp.zeros((1, 2 * TILE), F32)

    dk_ref[...] = dk_acc[...].astype(LOW)
    dv_ref[...] = dv_acc[...].astype(LOW)


def attend_back(queries, keys_all, values, grad_mixed, mixed, lse, seq_pos, rows):
    count, width = queries.shape
    length = keys_all.shape[0]
    pairs = H // PAIR
    lanes = width // pairs
    offs = length // TILE
    causal = rows is not None
    col = lambda size: pl.BlockSpec((size, lanes), lambda pair, *_: (0, pair))
    in_specs = [col(count), col(length), col(length), col(count), col(count),
                pl.BlockSpec((1, PAIR, count), lambda pair, *_: (pair, 0, 0))]
    out_specs = [col(count), col(length), col(length)]
    out_shape = [
        jax.ShapeDtypeStruct((count, width), LOW),
        jax.ShapeDtypeStruct((length, width), LOW),
        jax.ShapeDtypeStruct((length, width), LOW),
    ]
    args = [queries, keys_all, values, grad_mixed, mixed, lse]
    scratch = [pltpu.VMEM((length, lanes), F32), pltpu.VMEM((length, lanes), F32)]
    if causal:
        row_spec = pl.BlockSpec((1, PAIR, offs, 2 * TILE), lambda pair, *_: (pair, 0, 0, 0))
        in_specs.append(row_spec)
        out_specs.append(row_spec)
        out_shape.append(jax.ShapeDtypeStruct((pairs, PAIR, offs, 2 * TILE), F32))
        args = [seq_pos] + args + [rows]
        scratch += [pltpu.VMEM((PAIR, offs, TILE, TILE), F32)] * 2
    work = H * count * length
    return pl.pallas_call(
        functools.partial(back_kernel, causal),
        grid_spec=pltpu.PrefetchScalarGridSpec(
            num_scalar_prefetch=1 if causal else 0,
            grid=(pairs,),
            in_specs=in_specs,
            out_specs=out_specs,
            scratch_shapes=scratch,
        ),
        out_shape=out_shape,
        cost_estimate=pl.CostEstimate(
            flops=work * 640 * 2, bytes_accessed=12 * length * width, transcendentals=work
        ),
        name="attend_causal_back" if causal else "attend_cross_back",
    )(*args)


def bucket_rows(buckets, length):
    offs = length // TILE
    place = jnp.arange(2 * TILE, dtype=jnp.int32)
    step = jnp.where(place < TILE, place, place - 2 * TILE)
    gap = (jnp.arange(offs, dtype=jnp.int32) * TILE)[:, None] + step[None, :]
    marks = jnp.arange(BUCKETS, dtype=jnp.int32)
    begins = jnp.sum((buckets[None, :] < marks[:, None]).astype(jnp.int32), 1)
    ends = jnp.sum((buckets[None, :] <= marks[:, None]).astype(jnp.int32), 1)
    hot = (gap[None] >= begins[:, None, None]) & (gap[None] < ends[:, None, None])
    return (gap, hot.astype(LOW))


def bit_plan():
    bits = []
    for axis in ("seq", "shard"):
        size = lax.axis_size(axis)
        assert size & (size - 1) == 0
        bits += [(axis, place) for place in reversed(range(size.bit_length() - 1))]
    return bits


def bit_orders(bits):
    ends = [0, len(bits) - 2, len(bits) - 1]
    rest = [place for place in range(len(bits)) if place not in ends]
    return (rest + ends, rest + [ends[1], ends[0], ends[2]])


def coords(bits):
    return [lax.rem(lax.axis_index(axis) // (1 << place), 2) for axis, place in bits]


def partner(bits, which):
    axis, place = bits[which]
    index = lax.axis_index(axis)
    mine = lax.rem(index // (1 << place), 2)
    return {axis: index + (1 - 2 * mine) * (1 << place)}


def greet(bits):
    barrier = pltpu.get_barrier_semaphore()
    for which in range(len(bits)):
        pl.semaphore_signal(
            barrier, inc=1, device_id=partner(bits, which), device_id_type=pl.DeviceIdType.MESH
        )
    pl.semaphore_wait(barrier, len(bits))


def send(bits, which, source, target, sems):
    copy = pltpu.make_async_remote_copy(
        src_ref=source,
        dst_ref=target,
        send_sem=sems[0],
        recv_sem=sems[1],
        device_id=partner(bits, which),
        device_id_type=pl.DeviceIdType.MESH,
    )
    copy.start()
    return copy


def gather_kernel(bits, count, *refs):
    sources, outs = refs[:count], refs[count : 2 * count]
    send_sem, recv_sem, own_sem = refs[2 * count :]
    steps = len(bits)
    place = coords(bits)
    orders = bit_orders(bits)
    owns = []
    for item in range(count):
        own = pltpu.make_async_copy(sources[item], outs[item].at[tuple(place)], own_sem.at[item])
        own.start()
        owns.append(own)
    greet(bits)
    copies = {}
    for turn in range(steps + (count - 1) // 2):
        for item in range(count):
            step = turn - item // 2
            if not 0 <= step < steps:
                continue
            order = orders[item % 2]
            here = tuple(
                slice(None) if which in order[:step] else place[which] for which in range(steps)
            )
            target = outs[item].at[here]
            if step == 1:
                owns[item].wait()
            if step > 0:
                copies[item, step - 1].wait_recv()
            copies[item, step] = send(
                bits,
                order[step],
                sources[item] if step == 0 else target,
                target,
                (send_sem.at[item, step], recv_sem.at[item, step]),
            )
    for item in range(count):
        copies[item, steps - 1].wait_recv()
    for copy in copies.values():
        copy.wait_send()


def gather(items, collective_id):
    bits = bit_plan()
    count = len(items)
    sems = pltpu.SemaphoreType.DMA((count, len(bits)))
    outs = pl.pallas_call(
        functools.partial(gather_kernel, bits, count),
        out_shape=[jax.ShapeDtypeStruct((2,) * len(bits) + x.shape, x.dtype) for x in items],
        in_specs=[pl.BlockSpec(memory_space=pltpu.VMEM)] * count,
        out_specs=[pl.BlockSpec(memory_space=pl.ANY)] * count,
        scratch_shapes=[sems, sems, pltpu.SemaphoreType.DMA((count,))],
        compiler_params=pltpu.CompilerParams(collective_id=collective_id, has_side_effects=True),
        name="gather_rows",
    )(*items)
    return [out.reshape((-1,) + x.shape) for out, x in zip(outs, items)]


def scatter_kernel(bits, count, *refs):
    steps = len(bits)
    sources, outs, work = refs[:count], refs[count : 2 * count], refs[2 * count : 3 * count]
    arrivals = refs[3 * count : (3 + steps) * count]
    load_sem, send_sem, recv_sem = refs[(3 + steps) * count :]
    place = coords(bits)
    orders = [list(reversed(order)) for order in bit_orders(bits)]
    loads = []
    for item in range(count):
        load = pltpu.make_async_copy(sources[item], work[item], load_sem.at[item])
        load.start()
        loads.append(load)
    greet(bits)
    copies = {}

    def add(item, step):
        order = orders[item % 2]
        free = [which for which in range(steps) if which not in order[: step + 1]]
        arrived = arrivals[item * steps + step]
        copies[item, step].wait_recv()
        if not free:
            outs[item][...] = work[item][tuple(place)].astype(F32) + arrived[...].astype(F32)
            return

        @pl.loop(0, 1 << len(free))
        def _(block):
            sub = [lax.rem(block // (1 << (len(free) - 1 - i)), 2) for i in range(len(free))]
            here = tuple(
                sub[free.index(which)] if which in free else place[which] for which in range(steps)
            )
            total = work[item][here].astype(F32) + arrived[tuple(sub)].astype(F32)
            work[item][here] = total.astype(work[item].dtype)

    for turn in range(steps + 1 + (count - 1) // 2):
        for item in range(count):
            step = turn - item // 2
            if not 0 <= step <= steps:
                continue
            if step == 0:
                loads[item].wait()
            else:
                add(item, step - 1)
            if step == steps:
                continue
            order = orders[item % 2]
            there = tuple(
                1 - place[which]
                if which == order[step]
                else (place[which] if which in order[:step] else slice(None))
                for which in range(steps)
            )
            copies[item, step] = send(
                bits,
                order[step],
                work[item].at[there],
                arrivals[item * steps + step],
                (send_sem.at[item, step], recv_sem.at[item, step]),
            )
    for copy in copies.values():
        copy.wait_send()


def scatter(items, collective_id):
    bits = bit_plan()
    steps = len(bits)
    count = len(items)
    sems = pltpu.SemaphoreType.DMA((count, steps))
    owners = 1 << steps
    items = [x.reshape((2,) * steps + (x.shape[0] // owners,) + x.shape[1:]) for x in items]
    tails = [x.shape[steps:] for x in items]
    arrivals = [
        pltpu.VMEM((2,) * (steps - 1 - step) + tail, x.dtype)
        for x, tail in zip(items, tails)
        for step in range(steps)
    ]
    return pl.pallas_call(
        functools.partial(scatter_kernel, bits, count),
        out_shape=[jax.ShapeDtypeStruct(tail, F32) for tail in tails],
        in_specs=[pl.BlockSpec(memory_space=pl.ANY)] * count,
        out_specs=[pl.BlockSpec(memory_space=pltpu.VMEM)] * count,
        scratch_shapes=[pltpu.VMEM(x.shape, x.dtype) for x in items]
        + arrivals
        + [pltpu.SemaphoreType.DMA((count,)), sems, sems],
        compiler_params=pltpu.CompilerParams(collective_id=collective_id, has_side_effects=True),
        name="scatter_rows",
    )(*items)


def dot_low(left, right):
    return contract(left, right, 1, 0)


def dot_left(left, right):
    return contract(left, right, 0, 0)


def dot_right(left, right):
    return contract(left, right, 1, 1)


def rms_norm(value, gain):
    return value * lax.rsqrt(jnp.mean(value * value, -1, keepdims=True) + EPSILON) * gain


def norm_back(value, gain, grad):
    return jax.vjp(rms_norm, value, gain)[1](grad)


def gated(gate, upper):
    return jax.nn.gelu(gate, approximate=True) * upper


def pad_rows(rows, dtype):
    return jnp.stack([jnp.pad(row.astype(dtype), (0, 128 - row.shape[0])) for row in rows] + [
        jnp.zeros((128,), dtype)
    ] * (8 - len(rows)))


def on_device(
    hidden_in,
    encoded,
    cotangent,
    buckets,
    self_query,
    self_key,
    self_value,
    self_out,
    cross_query,
    cross_key,
    cross_value,
    cross_out,
    ff_gate,
    ff_up,
    ff_down,
    norm_self,
    norm_cross,
    norm_ff,
    bias_table,
):
    owners = lax.axis_size("seq") * lax.axis_size("shard")
    seq_pos = lax.axis_index("seq")
    seq_row = seq_pos.reshape(1).astype(jnp.int32)
    low_side = seq_pos == 0
    both = ("seq", "shard")
    width = hidden_in.shape[2]
    own_low = hidden_in[0]
    enc_own = encoded[0]
    before_low = lax.ppermute(own_low, "seq", [(0, 1)])
    enc_other = lax.ppermute(enc_own, "seq", [(0, 1), (1, 0)])
    w_gate_up = lax.all_gather(jnp.concatenate([ff_gate, ff_up], 1), both, axis=0, tiled=True)
    w_down = lax.all_gather(ff_down, both, axis=0, tiled=True)

    small = pad_rows([norm_self, norm_cross, norm_ff, bias_table], LOW)
    gathered = gather(
        [small, self_query, self_key, self_value, self_out, cross_query, cross_key, cross_value,
         cross_out],
        1,
    )
    smalls = gathered[0]
    w_query, w_key, w_value, w_sout, w_cquery, w_ckey, w_cvalue, w_cout = [
        x.reshape(-1, width) for x in gathered[1:]
    ]
    gain_one, gain_two, gain_three = [
        smalls[:, i, : norm_self.shape[0]].reshape(-1).astype(F32) for i in range(3)
    ]
    table = smalls[:, 3, : bias_table.shape[0]].reshape(H, BUCKETS)

    hidden = own_low.astype(F32)
    count = hidden.shape[0]
    length = count * lax.axis_size("seq")
    gap, hot = bucket_rows(buckets, length)
    rows = jnp.einsum("hb,bof->hof", table, hot, preferred_element_type=F32)
    rows = jnp.where(gap[None] >= 0, rows, NEGATIVE).reshape(H // PAIR, PAIR, *gap.shape)

    low_half = jnp.where(low_side, own_low, before_low).astype(F32)
    first = rms_norm(hidden, gain_one).astype(LOW)
    first_all = jnp.concatenate([rms_norm(low_half, gain_one).astype(LOW), first], 0)
    enc_all = jnp.concatenate([enc_own, enc_other], 0)

    query = dot_low(first, w_query).astype(LOW)
    key = dot_low(first_all, w_key).astype(LOW)
    value = dot_low(first_all, w_value).astype(LOW)
    self_mixed, self_lse = attend(query, key, value, seq_row, rows)
    after_self = hidden + dot_low(self_mixed, w_sout)
    second = rms_norm(after_self, gain_two).astype(LOW)
    cross_q = dot_low(second, w_cquery).astype(LOW)
    cross_k = dot_low(enc_all, w_ckey).astype(LOW)
    cross_v = dot_low(enc_all, w_cvalue).astype(LOW)
    cross_mixed, cross_lse = attend(cross_q, cross_k, cross_v, None, None)
    after_cross = after_self + dot_low(cross_mixed, w_cout)
    third = rms_norm(after_cross, gain_three).astype(LOW)
    hidden_units = ff_gate.shape[1]
    gate_up = dot_low(third, w_gate_up)
    gate, upper = gate_up[:, :hidden_units], gate_up[:, hidden_units:]
    inner = gated(gate, upper).astype(LOW)
    hidden_out = (after_cross + dot_low(inner, w_down)).astype(LOW)

    grad_top = cotangent[0]
    grad_wdown = dot_left(inner, grad_top).astype(LOW)
    grad_inner = dot_right(grad_top, w_down)
    grad_gate, grad_upper = jax.vjp(gated, gate, upper)[1](grad_inner)
    grads_low = jnp.concatenate([grad_gate.astype(LOW), grad_upper.astype(LOW)], 1)
    grad_wgate_up = dot_left(third, grads_low).astype(LOW)
    sum_gate_up = lax.psum_scatter(grad_wgate_up, both, scatter_dimension=0, tiled=True)
    grad_third = dot_right(grads_low, w_gate_up)
    norm_grad, grad_gain_three = norm_back(after_cross, gain_three, grad_third)
    grad_cross_res = grad_top.astype(F32) + norm_grad
    cross_res_low = grad_cross_res.astype(LOW)
    grad_wcout = dot_left(cross_mixed, cross_res_low).astype(LOW)
    grad_cross_mix = dot_right(cross_res_low, w_cout).astype(LOW)
    grad_cq, grad_ck, grad_cv = attend_back(
        cross_q, cross_k, cross_v, grad_cross_mix, cross_mixed, cross_lse, None, None
    )
    grad_enc = dot_right(grad_ck, w_ckey) + dot_right(grad_cv, w_cvalue)
    enc_back = lax.ppermute(grad_enc[count:].astype(LOW), "seq", [(0, 1), (1, 0)])
    grad_wcquery = dot_left(second, grad_cq).astype(LOW)
    grad_wckey = dot_left(enc_all, grad_ck).astype(LOW)
    grad_wcvalue = dot_left(enc_all, grad_cv).astype(LOW)
    norm_grad, grad_gain_two = norm_back(after_self, gain_two, dot_right(grad_cq, w_cquery))
    grad_self_res = grad_cross_res + norm_grad
    self_res_low = grad_self_res.astype(LOW)
    grad_wsout = dot_left(self_mixed, self_res_low).astype(LOW)
    grad_self_mix = dot_right(self_res_low, w_sout).astype(LOW)
    grad_q, grad_k, grad_v, grad_rows = attend_back(
        query, key, value, grad_self_mix, self_mixed, self_lse, seq_row, rows
    )
    grad_part = dot_right(grad_k, w_key) + dot_right(grad_v, w_value)
    part_back = lax.ppermute(grad_part[:count].astype(LOW), "seq", [(1, 0)])
    grad_wquery = dot_left(first, grad_q).astype(LOW)
    grad_wkey = dot_left(first_all, grad_k).astype(LOW)
    grad_wvalue = dot_left(first_all, grad_v).astype(LOW)
    grad_first = (
        dot_right(grad_q, w_query)
        + grad_part[count:]
        + jnp.where(low_side, grad_part[:count], 0.0)
        + part_back.astype(F32)
    )
    norm_grad, grad_gain_one = norm_back(hidden, gain_one, grad_first)
    grad_hidden = (grad_self_res + norm_grad).astype(LOW)
    grad_encoded = (grad_enc[:count] + enc_back.astype(F32)).astype(LOW)
    table_grad = jnp.einsum(
        "hof,bof->hb", grad_rows.reshape(H, *gap.shape), hot.astype(F32),
        precision=lax.Precision.HIGHEST,
    )
    small_grads = jnp.stack(
        [
            jnp.pad(x.reshape(owners, -1), ((0, 0), (0, 128 - x.size // owners)))
            for x in (grad_gain_one, grad_gain_two, grad_gain_three, table_grad)
        ]
        + [jnp.zeros((owners, 128), F32)] * 4,
        1,
    ).reshape(owners * 8, 128)
    sums = scatter(
        [grad_wdown, grad_wcout, grad_wcquery, grad_wckey, grad_wcvalue, grad_wsout, grad_wquery,
         grad_wkey, grad_wvalue, small_grads],
        2,
    )
    small_sum = sums[9]
    gains = norm_self.shape[0]
    return (
        hidden_out[None],
        grad_hidden[None],
        grad_encoded[None],
        sums[6],
        sums[7],
        sums[8],
        sums[5],
        sums[2],
        sums[3],
        sums[4],
        sums[1],
        sum_gate_up[:, :hidden_units].astype(F32),
        sum_gate_up[:, hidden_units:].astype(F32),
        sums[0],
        small_sum[0, :gains],
        small_sum[1, :gains],
        small_sum[2, :gains],
        small_sum[3, : bias_table.shape[0]],
    )


def solution(mesh):
    rows = P(("seq", "shard"), None)
    flat = P(("seq", "shard"))
    tokens = P("shard", "seq", None)
    return jax.shard_map(
        on_device,
        mesh=mesh,
        in_specs=(tokens,) * 3 + (P(),) + (rows,) * 11 + (flat,) * 4,
        out_specs=(tokens,) * 3 + (rows,) * 11 + (flat,) * 4,
        check_vma=False,
    )
```

time: 1910 us -> 437 us (0.23)
  waiting for transfers between devices: 1050 us -> 0.08 us
  Pallas kernels: 0 us -> 257 us
  local copies, waits for them, and re-layouts: 246 us -> 25.3 us
  matrix products: 283 us -> 109 us
  blocking collectives: 157 us -> 0 us
  other arithmetic: 114 us -> 10.3 us
    reduce_scatter x9 -> x1, waiting for transfers between devices: 674 us -> 0.01 us  [on_device(): lax.psum_scatter(grad_wgate_up, both, scatter_dimension=0, tiled=True)]
    pallas_call x0 -> x6, Pallas kernels: none -> 257 us  [the longest x1 100 us: gather(): pl.pallas_call(functools.partial(gather_kernel, bits, count), out_shape=[...]
    dot_general x61 -> x32, matrix products: 283 us -> 109 us  [the longest x30 109 us: contract(): lax.dot_general(left, right, (((left_dim,), (right_dim,)), ((), ())), pre...]
    unnamed x24 -> x3, waiting for transfers between devices: 156 us -> 0.05 us
    all_gather x11 -> x2, waiting for transfers between devices: 135 us -> 0.02 us  [the longest x1 0.02 us: on_device(): lax.all_gather(jnp.concatenate([ff_gate, ff_up], 1), both, axis=0, tiled=...]
    all_to_all x6 -> x0, waiting for transfers between devices: 88.6 us -> none  [the longest x1 39.2 us: on_device(): lax.all_to_all(packed_cross, 'seq', split_axis=2, concat_axis=1, tiled=True)]
    unnamed x2 -> x0, blocking collectives: 81.7 us -> none
    sub x2 -> x0, local copies, waits for them, and re-layouts: 81.6 us -> none  [scores_of(): bucket_hot = reached - beyond]
  transfers between devices with their start and end apart: 28 -> 7, of which waited for: 17 -> 0; matrix products, arithmetic and copies ran while one was open for 32% -> 23% of each run, Pallas kernels for 0% -> 59%
where the time goes in v1:
time: 437 us; the launch traced here: 438 us
  Pallas kernels  257 us (59%)
  matrix products  109 us (25%)
  local copies, waits for them, and re-layouts  25.3 us (6%)
  starting transfers between devices  21.4 us (5%)
  between operations  14.6 us (3%)
  other arithmetic  10.3 us (2%)
    dot_general x30, matrix products, contract(): lax.dot_general(left, right, (((left_dim,), (right_dim,)), ((), ())), pre...  109 us
    pallas_call x1, Pallas kernels, gather(): pl.pallas_call(functools.partial(gather_kernel, bits, count), out_shape=[...  100 us
    pallas_call x1, Pallas kernels, scatter(): pl.pallas_call(functools.partial(scatter_kernel, bits, count), out_shape=...  86.1 us
    pallas_call x2, Pallas kernels, attend(): pl.pallas_call(functools.partial(attend_kernel, causal), grid_spec=pltpu....  35.4 us
    pallas_call x2, Pallas kernels, attend_back(): pl.pallas_call(functools.partial(back_kernel, causal), grid_spec=pltpu.Pr...  35.3 us
    unnamed x117, local copies, waits for them, and re-layouts  14.7 us
    ppermute x1, starting transfers between devices, on_device(): lax.ppermute(grad_enc[count:].astype(LOW), 'seq', [(0, 1), (1, 0)])  14.6 us
  transfers between devices with their start and end apart: 7, of which 0 were waited for; matrix products, arithmetic and copies ran while one was open for 23% of the time, Pallas kernels for 59%

profile of v1, /device:TPU:0, one launch (start us, length us, event | category | flops | bytes accessed | tf_op | source)
XLA Modules:
  0.0 438.1 jit_solution(11778033692311759088)
XLA Ops:
  9.0 4.9 %collective-permute-start = (bf16[512,768]{1,0:T(8,128)(2,1)}, bf16[512,768]{1,0:T(8,128)(2,1)S(1)}, u32[]{:S(2)}, u32[]{:S(2)}) collective-permute-start(bf16[512,768]{1,0:T(8,128)(2,1)} %bitcast.116), channel_id=1, source_target_pairs={{0,16},{1,17},{2,18},{3,19},{4,20},{5,21},{6,22},{7,23},{8,24},{9,... | collective-permute-start | bytes 2359304 | tf_op jit(solution)/shard_map/ppermute | solution.py:540
  16.1 100.1 %gather_rows.1 = (bf16[2,2,2,2,2,8,128]{6,5,4,3,2,1,0:T(8,128)(2,1)}, bf16[2,2,2,2,2,24,768]{6,5,4,3,2,1,0:T(8,128)(2,1)}, bf16[2,2,2,2,2,24,768]{6,5,4,3,2,1,0:...) custom-call(bf16[8,128]{1,0:T(8,128)(2,1)} %stack.41.refs_0_, ...), custom_call_target="tpu_custom_call" | custom-call | tf_op jit(solution)/shard_map/gather_rows/pallas_call | solution.py:381
  124.0 2.6 convolution_convert_fusion.4.refs_3_
  126.6 2.6 convolution_convert_fusion.5.refs_2_
  129.2 16.0 %attend_causal.1 = (bf16[512,768]{1,0:T(8,128)(2,1)}, f32[6,2,512]{2,1,0:T(2,128)}) custom-call(s32[1]{0:T(128)} %bitcast.1.refs_0_, bf16[512,768]{1,0:T(8,128)(2,1)} %convolution_convert_fusion.17.refs_1_, bf16[1024,768]{1,0:T(8,128)(2,1)} %convolution_convert_fusion.5.refs_2_, bf16[1024,768]{1,0:T(8,128)(2,1)} %convolution_convert_fusion.4.refs_3_, ...), custom_call_target="tpu_custom_call" | custom-call | flops 3221225472 | bytes 4718592 | tf_op jit(solution)/shard_map/attend_causal/pallas_call | solution.py:126
  149.9 3.9 convolution_convert_fusion.2.refs_2_
  153.8 3.7 convolution_convert_fusion.3.refs_1_
  157.5 19.4 %attend_cross.1 = (bf16[512,768]{1,0:T(8,128)(2,1)}, f32[6,2,512]{2,1,0:T(2,128)}) custom-call(bf16[512,768]{1,0:T(8,128)(2,1)} %convolution_convert_fusion.16.refs_0_, bf16[1024,768]{1,0:T(8,128)(2,1)} %convolution_convert_fusion.3.refs_1_, bf16[1024,768]{1,0:T(8,128)(2,1)} %convolution_convert_fusion.2.refs_2_), custom_call_target="tpu_custom_call" | custom-call | flops 3221225472 | bytes 4718592 | tf_op jit(solution)/shard_map/attend_cross/pallas_call | solution.py:126
  179.3 8.6 %fusion.50 = f32[512,4096]{1,0:T(8,128)} fusion(bf16[768,4096]{1,0:T(8,128)(2,1)} %all-gather.3.cloned.1.call-done, f32[512,768]{1,0:T(8,128)S(1)} %get-tuple-element.104, f32[768]{0:T(1024)S(1)} %reshape.288, f32[512]{0:T(512)S(1)} %fusion.47), kind=kOutput, calls=%fused_computation.136 | convolution fusion | flops 3222405120 | bytes 16258048 | tf_op jit(solution)/shard_map/dot_general | solution.py:20
  187.9 21.6 %fusion.6 = (bf16[512,2048]{1,0:T(8,128)(2,1)S(1)}, bf16[512,2048]{1,0:T(8,128)(2,1)S(1)}, bf16[512,2048]{1,0:T(8,128)(2,1)}) fusion(f32[512,4096]{1,0:T(8,128)} %fusion.50, bf16[2048,768]{1,0:T(8,128)(2,1)} %all-gather.5.cloned.1.call-done, bf16[1,512,768]{2,1,0:T(8,128)(2,1)} %param.21), kind=kOutput, calls=%fused_computation.9 | convolution fusion | flops 1637875712 | bytes 18612224 | tf_op jit(solution)/shard_map/dot_general | solution.py:20
  211.5 5.6 %convolution_convert_fusion = bf16[768,4096]{1,0:T(8,128)(2,1)} fusion(bf16[512,2048]{1,0:T(8,128)(2,1)S(1)} %get-tuple-element.89, bf16[512,2048]{1,0:T(8,128)(2,1)S(1)} %get-tuple-element.88, f32[512,768]{1,0:T(8,128)S(1)} %get-tuple-element.104, f32[768]{0:T(1024)S(1)} %reshape.288, f32[512]{0:T(512)S(1)} %fusion.47), kind=kOutput, calls=%fused_computation | convolution fusion | flops 3233939456 | bytes 12063744 | tf_op jit(solution)/shard_map/dot_general | solution.py:20
  217.2 7.4 %multiply_reduce_fusion = (f32[768]{0:T(1024)S(1)}, f32[512]{0:T(512)S(1)}, f32[512,768]{1,0:T(8,128)S(1)}) fusion(f32[512,768]{1,0:T(8,128)S(1)} %get-tuple-element.104, f32[512]{0:T(512)S(1)} %fusion.47, f32[768]{0:T(1024)S(1)} %reshape.288, bf16[768,4096]{1,0:T(8,128)(2,1)} %all-gather.3.cloned.1.call-done, bf16[512,2048]{1,0:T(8,128)(2,1)} %copy-done.15, ...), kind=kOutput, calls=%fused_computation.53 | convolution fusion | flops 3231972096 | bytes 13641728 | tf_op jit(solution)/shard_map/dot_general | solution.py:20
  227.7 18.9 %attend_cross_back.1 = (bf16[512,768]{1,0:T(8,128)(2,1)}, bf16[1024,768]{1,0:T(8,128)(2,1)}, bf16[1024,768]{1,0:T(8,128)(2,1)}) custom-call(bf16[512,768]{1,0:T(8,128)(2,1)} %convolution_convert_fusion.16.refs_0_, bf16[1024,768]{1,0:T(8,128)(2,1)} %convolution_convert_fusion.3.refs_1_, bf16[1024,768]{1,0:T(8,128)(2,1)} %convolution_convert_fusion.2.refs_2_, ...), custom_call_target="tpu_custom_call" | custom-call | flops 8053063680 | bytes 9437184 | tf_op jit(solution)/shard_map/attend_cross_back/pallas_call | solution.py:260
  246.6 2.7 multiply_reduce_fusion.1
  252.4 16.4 %attend_causal_back.1 = (bf16[512,768]{1,0:T(8,128)(2,1)}, bf16[1024,768]{1,0:T(8,128)(2,1)}, bf16[1024,768]{1,0:T(8,128)(2,1)}, f32[6,2,4,512]{3,2,1,0:T(4,128)}) custom-call(s32[1]{0:T(128)} %bitcast.1.refs_0_, bf16[512,768]{1,0:T(8,128)(2,1)} %convolution_convert_fusion.17.refs_1_, bf16[1024,768]{1,0:T(8,128)(2,1)} %convolution_convert_fusion.5.refs_2_, ...), custom_call_target="tpu_custom_call" | custom-call | flops 8053063680 | bytes 9437184 | tf_op jit(solution)/shard_map/attend_causal_back/pallas_call | solution.py:260
  268.8 3.3 fusion.52
  278.6 3.3 fusion.53
  284.4 14.6 %collective-permute-start.3 = (bf16[512,768]{1,0:T(8,128)(2,1)}, bf16[512,768]{1,0:T(8,128)(2,1)}, u32[]{:S(2)}, u32[]{:S(2)}) collective-permute-start(bf16[512,768]{1,0:T(8,128)(2,1)} %slice.111), channel_id=1, source_target_pairs={{0,16},{16,0},{1,17},{17,1},{2,18},{18,2},{3,19},{19,3},{4,20},{20... | collective-permute-start | bytes 2359304 | tf_op jit(solution)/shard_map/ppermute | solution.py:607
  309.9 3.6 convolution_convert_fusion.11
  313.5 3.8 convolution_convert_fusion.10
  317.3 3.7 convolution_convert_fusion.1
  323.1 2.7 fusion.24
  329.3 86.1 %scatter_rows.1 = (f32[64,768]{1,0:T(8,128)}, f32[24,768]{1,0:T(8,128)}, f32[24,768]{1,0:T(8,128)}, f32[24,768]{1,0:T(8,128)}, f32[24,768]{1,0:T(8,128)}, /*inde...) custom-call(bf16[2,2,2,2,2,64,768]{6,5,4,3,2,1,0:T(8,128)(2,1)} %bitcast.119, ...), custom_call_target="tpu_custom_call" | custom-call | tf_op jit(solution)/shard_map/scatter_rows/pallas_call | solution.py:468
  418.0 2.8 fusion.27
  (196 shorter events, 65.1 us)
Async XLA Ops:
  7.2 113.3 %copy-start.4 = (bf16[1,512,768]{2,1,0:T(8,128)(2,1)S(1)}, bf16[1,512,768]{2,1,0:T(8,128)(2,1)}, u32[]{:S(2)}) copy-start(bf16[1,512,768]{2,1,0:T(8,128)(2,1)} %param.19) | copy-start | bytes 2359300
  7.2 172.1 %all-gather.3.cloned.1.call-start = ((), (), s32[]{:S(2)}) async-start(), calls=%async_computation.1 | async-start | bytes 6488064 | tf_op jit(solution)/shard_map/all_gather | solution.py:542
  9.0 178.9 %all-gather.5.cloned.1.call-start = ((), (), s32[]{:S(2)}) async-start(), calls=%async_computation.2 | async-start | bytes 3244032 | tf_op jit(solution)/shard_map/all_gather | solution.py:543
  9.0 111.5 %collective-permute-start = (bf16[512,768]{1,0:T(8,128)(2,1)}, bf16[512,768]{1,0:T(8,128)(2,1)S(1)}, u32[]{:S(2)}, u32[]{:S(2)}) collective-permute-start(bf16[512,768]{1,0:T(8,128)(2,1)} %bitcast.116), channel_id=1, source_target_pairs={{0,16},{1,17},{2,18},{3,19},{4,20},{5,21},{6,22},{7,23},{8,24},{9,... | collective-permute-start | bytes 2359304 | tf_op jit(solution)/shard_map/ppermute | solution.py:540
  13.9 135.4 %collective-permute-start.1 = (bf16[512,768]{1,0:T(8,128)(2,1)}, bf16[512,768]{1,0:T(8,128)(2,1)}, u32[]{:S(2)}, u32[]{:S(2)}) collective-permute-start(bf16[512,768]{1,0:T(8,128)(2,1)} %bitcast.150), channel_id=1, source_target_pairs={{0,16},{16,0},{1,17},{17,1},{2,18},{18,2},{3,19},{19,3},{4,20},{20... | collective-permute-start | bytes 2359304 | tf_op jit(solution)/shard_map/ppermute | solution.py:541
  14.1 408.0 %reduce-scatter.2.cloned.1.call-start = ((), (), s32[]{:S(2)}) async-start(), calls=%async_computation.3 | async-start | bytes 6488064 | tf_op jit(solution)/shard_map/reduce_scatter | solution.py:596
  116.2 4.8 %copy-start.39 = (bf16[2,2,2,2,2,24,768]{6,5,4,3,2,1,0:T(8,128)(2,1)S(1)}, bf16[2,2,2,2,2,24,768]{6,5,4,3,2,1,0:T(8,128)(2,1)}, u32[]{:S(2)}) copy-start(bf16[2,2,2,2,2,24,768]{6,5,4,3,2,1,0:T(8,128)(2,1)} %get-tuple-element.49) | copy-start | bytes 3538948
  129.2 16.0 %copy-start.43 = (bf16[2,2,2,2,2,24,768]{6,5,4,3,2,1,0:T(8,128)(2,1)S(1)}, bf16[2,2,2,2,2,24,768]{6,5,4,3,2,1,0:T(8,128)(2,1)}, u32[]{:S(2)}) copy-start(bf16[2,2,2,2,2,24,768]{6,5,4,3,2,1,0:T(8,128)(2,1)} %get-tuple-element.53) | copy-start | bytes 3538948
  149.9 3.9 copy-start.41
  157.5 19.4 %copy-start.8 = (f32[512,768]{1,0:T(8,128)S(1)}, f32[512,768]{1,0:T(8,128)}, u32[]{:S(2)}) copy-start(f32[512,768]{1,0:T(8,128)} %copy-done.7) | copy-start | bytes 4718596
  217.2 7.4 %copy-start.29 = (bf16[1,512,768]{2,1,0:T(8,128)(2,1)S(1)}, bf16[1,512,768]{2,1,0:T(8,128)(2,1)}, u32[]{:S(2)}) copy-start(bf16[1,512,768]{2,1,0:T(8,128)(2,1)} %param.21) | copy-start | bytes 2359300
  276.2 49.6 %collective-permute-start.2 = (bf16[512,768]{1,0:T(8,128)(2,1)}, bf16[512,768]{1,0:T(8,128)(2,1)}, u32[]{:S(2)}, u32[]{:S(2)}) collective-permute-start(bf16[512,768]{1,0:T(8,128)(2,1)} %slice.112), channel_id=1, source_target_pairs={{16,0},{17,1},{18,2},{19,3},{20,4},{21,5},{22,6},{23,7},{24,8},{25... | collective-permute-start | bytes 2359304 | tf_op jit(solution)/shard_map/ppermute | solution.py:620
  283.4 17.5 %copy-start.3 = (f32[1024,768]{1,0:T(8,128)}, f32[1024,768]{1,0:T(8,128)S(1)}, u32[]{:S(2)}) copy-start(f32[1024,768]{1,0:T(8,128)S(1)} %convolution_add_fusion) | copy-start | bytes 9437188
  283.4 15.6 %copy-start.24 = (bf16[512,768]{1,0:T(8,128)(2,1)S(1)}, bf16[512,768]{1,0:T(8,128)(2,1)}, u32[]{:S(2)}) copy-start(bf16[512,768]{1,0:T(8,128)(2,1)} %get-tuple-element.52.refs_5_) | copy-start | bytes 2359300
  284.4 16.5 %copy-start.2 = (f32[512,768]{1,0:T(8,128)S(1)}, f32[512,768]{1,0:T(8,128)}, u32[]{:S(2)}) copy-start(f32[512,768]{1,0:T(8,128)} %copy-done) | copy-start | bytes 4718596
  284.4 16.5 %copy-start.13 = (bf16[512,768]{1,0:T(8,128)(2,1)S(1)}, bf16[512,768]{1,0:T(8,128)(2,1)}, u32[]{:S(2)}) copy-start(bf16[512,768]{1,0:T(8,128)(2,1)} %get-tuple-element.57.refs_4_) | copy-start | bytes 2359300
  284.4 133.6 %collective-permute-start.3 = (bf16[512,768]{1,0:T(8,128)(2,1)}, bf16[512,768]{1,0:T(8,128)(2,1)}, u32[]{:S(2)}, u32[]{:S(2)}) collective-permute-start(bf16[512,768]{1,0:T(8,128)(2,1)} %slice.111), channel_id=1, source_target_pairs={{0,16},{16,0},{1,17},{17,1},{2,18},{18,2},{3,19},{19,3},{4,20},{20... | collective-permute-start | bytes 2359304 | tf_op jit(solution)/shard_map/ppermute | solution.py:607
  420.7 6.2 %copy-start.37 = (f32[24,768]{1,0:T(8,128)S(1)}, f32[24,768]{1,0:T(8,128)}, u32[]{:S(2)}) copy-start(f32[24,768]{1,0:T(8,128)} %get-tuple-element.135) | copy-start | bytes 221188
  420.7 6.8 %copy-start.36 = (f32[24,768]{1,0:T(8,128)S(1)}, f32[24,768]{1,0:T(8,128)}, u32[]{:S(2)}) copy-start(f32[24,768]{1,0:T(8,128)} %get-tuple-element.136) | copy-start | bytes 221188
  420.7 7.4 %copy-start.35 = (f32[24,768]{1,0:T(8,128)S(1)}, f32[24,768]{1,0:T(8,128)}, u32[]{:S(2)}) copy-start(f32[24,768]{1,0:T(8,128)} %get-tuple-element.137) | copy-start | bytes 221188
  420.7 8.1 %copy-start.34 = (f32[24,768]{1,0:T(8,128)S(1)}, f32[24,768]{1,0:T(8,128)}, u32[]{:S(2)}) copy-start(f32[24,768]{1,0:T(8,128)} %get-tuple-element.138) | copy-start | bytes 221188
  420.7 8.7 %copy-start.33 = (f32[24,768]{1,0:T(8,128)S(1)}, f32[24,768]{1,0:T(8,128)}, u32[]{:S(2)}) copy-start(f32[24,768]{1,0:T(8,128)} %get-tuple-element.139) | copy-start | bytes 221188
  422.1 8.0 %copy-start.32 = (f32[24,768]{1,0:T(8,128)S(1)}, f32[24,768]{1,0:T(8,128)}, u32[]{:S(2)}) copy-start(f32[24,768]{1,0:T(8,128)} %get-tuple-element.140) | copy-start | bytes 221188
  422.1 8.6 %copy-start.31 = (f32[64,768]{1,0:T(8,128)S(1)}, f32[64,768]{1,0:T(8,128)}, u32[]{:S(2)}) copy-start(f32[64,768]{1,0:T(8,128)} %get-tuple-element.143) | copy-start | bytes 589828
  (37 other events, 91.6 us)
Sparse Core Ops, SparseCore 0:
  11.5 89.2 all-gather.2
  103.6 59.1 all-gather.4
  217.3 120.8 reduce-scatter.1
